TPU v7x, 32 devices: a whole 2x2x4 slice. The times are simulated.
32 devices in a mesh: segment: 4 (over y, core), shard: 8 (over z, x).
Axes of the slice: x: 2, y: 2, z: 4, core: 2. Of those that a mesh axis runs over, the one named last changes fastest.
Arguments:
- buffer: bfloat16 [8, 18432, 2304], P('segment', 'shard'), may hold values from -6 to 6
- right_basis: bfloat16 [8, 2304, 256], P('segment', 'shard'), may hold values from -0.125 to 0.125
- layer_count: int32 [4], P('segment'), may hold values from 1 to 2, as said below
Outputs:
- momentum_out: bfloat16 [8, 18432, 2304], P('segment', 'shard')
- left_step: bfloat16 [8, 18432, 256], P('segment', 'shard')
- right_step: float32 [8, 2304, 256], P('segment', 'shard')
Inputs may be any that keep to these rules, and one draw needn't show every extreme that they name: `layer_count`: each segment uses between 1 and 2 slots; some segment uses 2 and some segment uses 1.
All inputs are finite; a program needn't handle non-finite values.
Results may differ from a plain program's by a relative error of at most 0.0024.
Values may be sent and summed in bfloat16 or wider, within the bound.
A program may use at most 128 MiB of HBM per device.

v0:
```python
import math
import jax
import jax.numpy as jnp
from jax import lax
from jax.sharding import PartitionSpec as P

MOMENTUM = 0.9
CLIP_RMS = 0.35
SQUARE_FLOOR = 0.0625


def finish_basis(proj, gram):
    lower = jnp.linalg.cholesky(gram)
    solved = jax.scipy.linalg.solve_triangular(lower, jnp.swapaxes(proj, 1, 2), lower=True)
    return jnp.swapaxes(solved, 1, 2)


def right_factor(partial_value):
    groups = lax.axis_size("shard")
    cols = partial_value.shape[1]
    width = cols // groups
    full = lax.psum(partial_value, "shard")
    colsq = jnp.sum(full * full, axis=1, keepdims=True)
    scaled = full * (math.sqrt(cols) * lax.rsqrt(colsq + 1.0))
    local = lax.dynamic_slice_in_dim(scaled, lax.axis_index("shard") * width, width, 1)
    return (full.astype(jnp.bfloat16), local)


def finish_layers(block, proj, gram, used, clip, rows_all):
    ortho = finish_basis(proj, gram)
    half_left = ortho.astype(jnp.bfloat16)
    partial_value = jnp.einsum("kij,kir->kjr", block, half_left, preferred_element_type=jnp.float32)
    half_right, right_local = right_factor(partial_value)
    correction = jnp.einsum(
        "kir,kjr->kij", half_left, half_right, preferred_element_type=jnp.float32
    )
    keep = used[:, None, None]
    moment = jnp.where(keep, block - (1.0 - MOMENTUM) * correction, 0.0).astype(jnp.bfloat16)
    left = jnp.where(keep, clip * math.sqrt(rows_all) * ortho, 0.0).astype(jnp.bfloat16)
    right = jnp.where(keep, right_local, 0.0)
    return (moment, left, right)


def body(buffer, right_basis, layer_count):
    slots = buffer.shape[0]
    rows_dev = buffer.shape[1]
    cols = buffer.shape[2]
    rows_all = rows_dev * lax.axis_size("shard")
    count = layer_count[0]
    used = jnp.arange(slots, dtype=jnp.int32) < count
    per_slot = jnp.sum(jnp.square(buffer.astype(jnp.float32)), axis=(1, 2))
    local_sq = jnp.sum(jnp.where(used, per_slot, 0.0))
    local_elems = count.astype(jnp.float32) * float(rows_dev * cols)
    total_sq, total_elems = lax.psum((local_sq, local_elems), ("segment", "shard"))
    clip = jnp.minimum(1.0, CLIP_RMS * lax.rsqrt(jnp.maximum(total_sq / total_elems, SQUARE_FLOOR)))
    proj = jnp.einsum(
        "kij,kjr->kir",
        buffer,
        lax.all_gather(right_basis, "shard", axis=1, tiled=True),
        preferred_element_type=jnp.float32,
    )
    local_gram = jnp.einsum("kir,kis->krs", proj, proj, precision=lax.Precision.HIGHEST)
    gram = lax.psum(local_gram, "shard")
    return finish_layers(buffer, proj, gram, used, clip, rows_all)


def solution(mesh):
    in_specs = (P("segment", "shard", None), P("segment", "shard", None), P("segment"))
    out_specs = (
        P("segment", "shard", None),
        P("segment", "shard", None),
        P("segment", "shard", None),
    )
    return jax.shard_map(body, mesh=mesh, in_specs=in_specs, out_specs=out_specs, check_vma=False)
```

profile of v0, /device:TPU:0, one launch (start us, length us, event | category | flops | bytes accessed | tf_op | source)
XLA Modules:
  0.0 498.2 jit_solution(15562166234760625701)
XLA Ops:
  7.2 0.0 all-gather.2.cloned.1.call-start
  7.2 0.7 all-gather.2.cloned.1.call-update
  7.9 0.0 all-reduce.5.cloned.1.call-start
  7.9 56.8 %all-gather.2.cloned.1.call-done = bf16[2,2304,256]{2,1,0:T(8,128)(2,1)} async-done(((bf16[2,288,256]{2,1,0:T(8,128)(2,1)}), bf16[2,2304,256]{2,1,0:T(8,128)(2,1)}) %all-gather.2.cloned.1.call-update) | async-done | bytes 2359312 | tf_op jit(solution)/shard_map/all_gather | solution.py:59
  64.7 10.6 %fusion.20 = f32[2,2304,256]{2,1,0:T(8,128)S(1)} fusion(bf16[2,2304,2304]{2,1,0:T(8,128)(2,1)} %param.3, bf16[2,2304,256]{2,1,0:T(8,128)(2,1)} %all-gather.2.cloned.1.call-done), kind=kOutput, calls=%fused_computation.47 | convolution fusion | flops 5435817984 | bytes 28311552 | tf_op jit(solution)/shard_map/kij,kjr->kir/dot_general | solution.py:56
  75.4 0.0 copy-start
  75.4 2.2 copy-done
  77.6 8.4 %fusion.21 = f32[2,256,256]{1,2,0:T(8,128)} fusion(f32[2,2304,256]{2,1,0:T(8,128)S(1)} %fusion.20), kind=kOutput, calls=%fused_computation.48 | convolution fusion | flops 3623878656 | bytes 5242880 | tf_op jit(solution)/shard_map/kir,kis->krs/dot_general | solution.py:62
  86.0 0.0 all-reduce.5.cloned.1.call-update
  86.0 0.5 all-reduce.7.cloned.1.call-start
  86.6 70.8 %all-reduce.5.cloned.1.call-done = f32[2,256,256]{1,2,0:T(8,128)} async-done(((f32[2,256,256]{1,2,0:T(8,128)}), f32[2,256,256]{1,2,0:T(8,128)}) %all-reduce.5.cloned.1.call-update) | async-done | bytes 524304 | tf_op jit(solution)/shard_map/psum | solution.py:63
  157.4 1.2 copy.22
  158.7 1.1 fusion.9
  159.8 23.5 %custom-call.17 = f32[2,128,128]{2,1,0:T(8,128)S(1)} custom-call(f32[2,128,128]{2,1,0:T(8,128)S(1)} %cholesky.122), custom_call_target="Cholesky" | custom-call | tf_op jit(solution)/shard_map/jit(cholesky)/cholesky | solution.py:13
  183.3 19.7 %custom-call.18 = f32[2,1,128,128]{2,3,1,0:T(8,128)S(1)} custom-call(f32[2,1,128,128]{3,2,1,0:T(8,128)S(1)} %select_bitcast_fusion), custom_call_target="InvertDiagBlocksLowerTriangular" | custom-call | tf_op jit(solution)/shard_map/jit(cholesky)/cholesky | solution.py:13
  203.0 0.3 constant_dynamic-update-slice_fusion.1
  203.3 0.4 convolution_subtract_fusion.1
  203.7 23.5 %custom-call.19 = f32[2,128,128]{2,1,0:T(8,128)S(1)} custom-call(f32[2,128,128]{2,1,0:T(8,128)S(1)} %convolution_subtract_fusion.1), custom_call_target="Cholesky" | custom-call | tf_op jit(solution)/shard_map/jit(cholesky)/cholesky | solution.py:13
  227.2 0.2 compare_reduce_fusion
  227.3 0.1 select_select_fusion
  227.5 0.1 triangular_solve.62
  227.6 4.1 while.1
  227.6 0.6 fusion.32
  228.2 1.4 bitcast_dynamic-update-slice_fusion.2
  229.6 0.6 fusion.32
  230.2 1.4 bitcast_dynamic-update-slice_fusion.2
  231.7 39.5 %custom-call.20 = f32[2,2,128,128]{2,3,1,0:T(8,128)S(1)} custom-call(f32[2,2,128,128]{3,2,1,0:T(8,128)S(1)} %bitcast.52), custom_call_target="InvertDiagBlocksLowerTriangular" | custom-call | tf_op jit(solution)/shard_map/jit(_solve_triangular)/vmap()/triangular_solve | solution.py:14
  271.2 0.0 copy-start.1
  271.2 4.0 fusion.5
  275.2 0.0 copy-done.1
  275.2 3.9 convolution_subtract_fusion
  279.1 2.2 fusion.13
  281.3 0.0 copy-start.2
  281.4 1.4 copy-done.2
  282.8 12.2 %convolution_bitcast_fusion = f32[2,2304,256]{1,2,0:T(8,128)} fusion(bf16[2,2304,2304]{2,1,0:T(8,128)(2,1)} %param.3, f32[2,128,2304]{2,1,0:T(8,128)S(1)} %fusion.13, f32[2,128,2304]{2,1,0:T(8,128)S(1)} %fusion.5), kind=kOutput, calls=%fused_computation.7 | convolution fusion | flops 5440536576 | bytes 30670848 | tf_op jit(solution)/shard_map/kij,kir->kjr/dot_general | solution.py:32
  295.0 0.0 all-reduce.7.cloned.1.call-update
  295.7 13.7 %fusion.2 = f32[2]{0:T(128)S(1)} fusion(bf16[2,2304,2304]{2,1,0:T(8,128)(2,1)} %param.3), kind=kLoop, calls=%fused_computation.6 | loop fusion | flops 31850494 | bytes 21233672 | tf_op jit(solution)/shard_map/reduce_sum | solution.py:51
  309.4 0.6 select_reduce_fusion.2
  310.0 43.1 %all-reduce.1 = (f32[]{:T(128)}, f32[]{:T(128)}) all-reduce(f32[]{:T(128)} %select_reduce_fusion.2, f32[]{:T(128)S(6)} %mul.46), channel_id=1, replica_groups=mesh['segment'=4,'shard'=8] {'segment','shard'}, use_global_device_ids=true, to_apply=%region_8.9 | all-reduce | flops 2 | bytes 16 | tf_op jit(solution)/shard_map/psum | solution.py:54
  354.5 3.6 fusion.4
  358.1 4.3 copy.32
  362.4 102.5 %all-reduce.7.cloned.1.call-done = f32[2,2304,256]{1,2,0:T(8,128)} async-done(((f32[2,2304,256]{1,2,0:T(8,128)}), f32[2,2304,256]{1,2,0:T(8,128)}) %all-reduce.7.cloned.1.call-update) | async-done | bytes 4718608 | tf_op jit(solution)/shard_map/psum | solution.py:22
  464.9 2.7 multiply_reduce_fusion
  467.6 1.6 fusion.8
  469.2 1.1 copy.33
  470.3 21.2 %fusion.1 = bf16[2,2304,2304]{2,1,0:T(8,128)(2,1)} fusion(bf16[2,2304,2304]{2,1,0:T(8,128)(2,1)} %param.3, pred[2]{0:T(512)(128)(4,1)S(1)} %iota_compare_fusion.3, f32[2,2304,256]{1,2,0:T(8,128)} %all-reduce.7.cloned.1.call-done, f32[2,128,2304]{2,1,0:T(8,128)} %copy-done.2, f32[2,128,2304]{2,1,0:T(8,128)S(1)} %fusion.5), kind=kOutput, calls=%fused_computation.5 | convolution fusion | flops 5494800384 | bytes 51904512 | tf_op jit(solution)/shard_map/kir,kjr->kij/dot_general | solution.py:34
  (14 shorter events, 0.2 us)
Async XLA Ops:
  7.2 57.6 %all-gather.2.cloned.1.call-start = ((), (), s32[]{:S(2)}) async-start(), calls=%async_computation | async-start | bytes 2654208 | tf_op jit(solution)/shard_map/all_gather | solution.py:59
  7.9 149.5 %all-reduce.5.cloned.1.call-start = ((), (), s32[]{:S(2)}) async-start(), calls=%async_computation.1 | async-start | bytes 1048576 | tf_op jit(solution)/shard_map/psum | solution.py:63
  75.4 2.2 copy-start
  86.0 378.9 %all-reduce.7.cloned.1.call-start = ((), (), s32[]{:S(2)}) async-start(), calls=%async_computation.2 | async-start | bytes 9437184 | tf_op jit(solution)/shard_map/psum | solution.py:22
  271.2 4.0 copy-start.1
  281.3 1.4 copy-start.2
Sparse Core Ops, SparseCore 0:
  10.2 54.5 all-gather.1
  86.1 71.2 all-reduce.4
  295.2 169.6 all-reduce.6
where the time goes:
time: 506 us; the launch traced here: 498 us
  waiting for transfers between devices  231 us (46%)
  other arithmetic  130 us (26%)
  matrix products  63.2 us (12%)
  blocking collectives  43.1 us (9%)
  between operations  16.2 us (3%)
  local copies, waits for them, and re-layouts  14.4 us (3%)
    psum x1, waiting for transfers between devices, right_factor(): full = lax.psum(partial_value, 'shard')  102 us
    psum x1, waiting for transfers between devices, body(): gram = lax.psum(local_gram, 'shard')  70.8 us
    another operation x9, other arithmetic, finish_basis(): lower = jnp.linalg.cholesky(gram)  66.8 us
    all_gather x1, waiting for transfers between devices, body(): lax.all_gather(right_basis, 'shard', axis=1, tiled=True)  56.8 us
    psum x1, blocking collectives, body(): lax.psum((local_sq, local_elems), ('segment', 'shard'))  43.1 us
    another operation x4, other arithmetic, finish_basis(): jax.scipy.linalg.solve_triangular(lower, jnp.swapaxes(proj, 1, 2), lower=...  39.7 us
    dot_general x1, matrix products, finish_layers(): jnp.einsum('kir,kjr->kij', half_left, half_right, preferred_element_type=...  21.2 us
    reduce_sum x1, other arithmetic, body(): per_slot = jnp.sum(jnp.square(buffer.astype(jnp.float32)), axis=(1, 2))  13.7 us
  transfers between devices with their start and end apart: 3, of which 3 were waited for; matrix products, arithmetic and copies ran while one was open for 4% of the time, Pallas kernels for 0%

commit v1 on v0

--- a/solution.py
+++ b/solution.py
@@ -60,7 +60,7 @@
         preferred_element_type=jnp.float32,
     )
     local_gram = jnp.einsum("kir,kis->krs", proj, proj, precision=lax.Precision.HIGHEST)
-    gram = lax.psum(local_gram, "shard")
+    gram = jnp.sum(lax.all_gather(local_gram, "shard"), axis=0)
     return finish_layers(buffer, proj, gram, used, clip, rows_all)
 
 

time: 506 us -> 507 us (level)
    all_gather x0 -> x1, waiting for transfers between devices: none -> 70.9 us  [body(): gram = jnp.sum(lax.all_gather(local_gram, 'shard'), axis=0)]
    psum x1 -> x0, waiting for transfers between devices: 70.8 us -> none  [body(): gram = lax.psum(local_gram, 'shard')]
where the time goes in v1:
time: 507 us; the launch traced here: 500 us
  waiting for transfers between devices  231 us (46%)
  other arithmetic  131 us (26%)
  matrix products  64.7 us (13%)
  blocking collectives  42.6 us (8%)
  between operations  16.2 us (3%)
  local copies, waits for them, and re-layouts  13.4 us (3%)
    psum x1, waiting for transfers between devices, right_factor(): full = lax.psum(partial_value, 'shard')  102 us
    all_gather x1, waiting for transfers between devices, body(): gram = jnp.sum(lax.all_gather(local_gram, 'shard'), axis=0)  70.9 us
    another operation x9, other arithmetic, finish_basis(): lower = jnp.linalg.cholesky(gram)  66.8 us
    all_gather x1, waiting for transfers between devices, body(): lax.all_gather(right_basis, 'shard', axis=1, tiled=True)  56.8 us
    psum x1, blocking collectives, body(): lax.psum((local_sq, local_elems), ('segment', 'shard'))  42.6 us
    another operation x4, other arithmetic, finish_basis(): jax.scipy.linalg.solve_triangular(lower, jnp.swapaxes(proj, 1, 2), lower=...  39.7 us
    dot_general x1, matrix products, finish_layers(): jnp.einsum('kir,kjr->kij', half_left, half_right, preferred_element_type=...  21.2 us
    reduce_sum x1, other arithmetic, body(): per_slot = jnp.sum(jnp.square(buffer.astype(jnp.float32)), axis=(1, 2))  13.7 us
  transfers between devices with their start and end apart: 3, of which 3 were waited for; matrix products, arithmetic and copies ran while one was open for 4% of the time, Pallas kernels for 0%

profile of v1, /device:TPU:0, one launch (start us, length us, event | category | flops | bytes accessed | tf_op | source)
XLA Modules:
  0.0 499.5 jit_solution(9257963927521960486)
XLA Ops:
  7.2 0.0 all-gather.4.cloned.1.call-start
  7.2 0.7 all-gather.4.cloned.1.call-update
  7.9 0.0 all-gather.6.cloned.1.call-start
  7.9 56.8 %all-gather.4.cloned.1.call-done = bf16[2,2304,256]{2,1,0:T(8,128)(2,1)} async-done(((bf16[2,288,256]{2,1,0:T(8,128)(2,1)}), bf16[2,2304,256]{2,1,0:T(8,128)(2,1)}) %all-gather.4.cloned.1.call-update) | async-done | bytes 2359312 | tf_op jit(solution)/shard_map/all_gather | solution.py:59
  64.7 10.6 %fusion.20 = f32[2,2304,256]{2,1,0:T(8,128)S(1)} fusion(bf16[2,2304,2304]{2,1,0:T(8,128)(2,1)} %param.3, bf16[2,2304,256]{2,1,0:T(8,128)(2,1)} %all-gather.4.cloned.1.call-done), kind=kOutput, calls=%fused_computation.47 | convolution fusion | flops 5435817984 | bytes 28311552 | tf_op jit(solution)/shard_map/kij,kjr->kir/dot_general | solution.py:56
  75.4 0.0 copy-start
  75.4 2.2 copy-done
  77.6 8.4 %fusion.21 = f32[2,256,256]{2,1,0:T(8,128)} fusion(f32[2,2304,256]{2,1,0:T(8,128)S(1)} %fusion.20), kind=kOutput, calls=%fused_computation.48 | convolution fusion | flops 3623878656 | bytes 5242880 | tf_op jit(solution)/shard_map/kir,kis->krs/dot_general | solution.py:62
  86.0 0.0 all-gather.6.cloned.1.call-update
  86.0 0.5 all-reduce.4.cloned.1.call-start
  86.7 70.9 %all-gather.6.cloned.1.call-done = f32[16,256,256]{2,1,0:T(8,128)} async-done(((f32[2,256,256]{2,1,0:T(8,128)}), f32[16,256,256]{2,1,0:T(8,128)}) %all-gather.6.cloned.1.call-update) | async-done | bytes 4194320 | tf_op jit(solution)/shard_map/all_gather | solution.py:63
  157.5 2.5 reduce_sum.36
  160.0 0.2 copy.33
  160.2 0.1 fusion.9
  160.3 23.5 %custom-call.17 = f32[2,128,128]{2,1,0:T(8,128)S(1)} custom-call(f32[2,128,128]{2,1,0:T(8,128)S(1)} %cholesky.122), custom_call_target="Cholesky" | custom-call | tf_op jit(solution)/shard_map/jit(cholesky)/cholesky | solution.py:13
  183.9 19.7 %custom-call.18 = f32[2,1,128,128]{2,3,1,0:T(8,128)S(1)} custom-call(f32[2,1,128,128]{3,2,1,0:T(8,128)S(1)} %select_bitcast_fusion), custom_call_target="InvertDiagBlocksLowerTriangular" | custom-call | tf_op jit(solution)/shard_map/jit(cholesky)/cholesky | solution.py:13
  203.5 0.3 constant_dynamic-update-slice_fusion.1
  203.8 0.4 convolution_subtract_fusion.1
  204.2 23.5 %custom-call.19 = f32[2,128,128]{2,1,0:T(8,128)S(1)} custom-call(f32[2,128,128]{2,1,0:T(8,128)S(1)} %convolution_subtract_fusion.1), custom_call_target="Cholesky" | custom-call | tf_op jit(solution)/shard_map/jit(cholesky)/cholesky | solution.py:13
  227.7 0.2 compare_reduce_fusion
  227.9 0.1 select_select_fusion
  228.0 0.1 triangular_solve.62
  228.1 4.1 while.1
  228.1 0.6 fusion.32
  228.7 1.4 bitcast_dynamic-update-slice_fusion.2
  230.2 0.6 fusion.32
  230.8 1.4 bitcast_dynamic-update-slice_fusion.2
  232.2 39.5 %custom-call.20 = f32[2,2,128,128]{2,3,1,0:T(8,128)S(1)} custom-call(f32[2,2,128,128]{3,2,1,0:T(8,128)S(1)} %bitcast.54), custom_call_target="InvertDiagBlocksLowerTriangular" | custom-call | tf_op jit(solution)/shard_map/jit(_solve_triangular)/vmap()/triangular_solve | solution.py:14
  271.7 3.8 fusion.5
  275.6 5.6 %convolution_subtract_fusion = f32[2,128,2304]{1,2,0:T(8,128)S(1)} fusion(f32[2,128,2304]{2,1,0:T(8,128)S(1)} %fusion.5, f32[2,256,2304]{1,2,0:T(8,128)} %bitcast.52, f32[2,256,256]{2,1,0:T(8,128)S(1)} %get-tuple-element.90), kind=kOutput, calls=%fused_computation.11 | convolution fusion | flops 906559488 | bytes 7208960 | tf_op jit(solution)/shard_map/jit(_solve_triangular)/vmap()/triangular_solve | solution.py:14
  281.1 2.2 fusion.13
  283.4 0.0 copy-start.1
  283.4 1.4 copy-done.1
  284.8 12.2 %convolution_bitcast_fusion = f32[2,2304,256]{1,2,0:T(8,128)} fusion(bf16[2,2304,2304]{2,1,0:T(8,128)(2,1)} %param.3, f32[2,128,2304]{2,1,0:T(8,128)S(1)} %fusion.13, f32[2,128,2304]{2,1,0:T(8,128)S(1)} %fusion.5), kind=kOutput, calls=%fused_computation.7 | convolution fusion | flops 5440536576 | bytes 30670848 | tf_op jit(solution)/shard_map/kij,kir->kjr/dot_general | solution.py:32
  297.1 0.0 all-reduce.4.cloned.1.call-update
  297.7 13.7 %fusion.2 = f32[2]{0:T(128)S(1)} fusion(bf16[2,2304,2304]{2,1,0:T(8,128)(2,1)} %param.3), kind=kLoop, calls=%fused_computation.6 | loop fusion | flops 31850494 | bytes 21233672 | tf_op jit(solution)/shard_map/reduce_sum | solution.py:51
  311.4 0.6 select_reduce_fusion.2
  312.0 42.6 %all-reduce.1 = (f32[]{:T(128)}, f32[]{:T(128)}) all-reduce(f32[]{:T(128)} %select_reduce_fusion.2, f32[]{:T(128)S(6)} %mul.46), channel_id=1, replica_groups=mesh['segment'=4,'shard'=8] {'segment','shard'}, use_global_device_ids=true, to_apply=%region_8.9 | all-reduce | flops 2 | bytes 16 | tf_op jit(solution)/shard_map/psum | solution.py:54
  356.0 3.6 fusion.4
  359.6 4.3 copy.44
  363.9 102.3 %all-reduce.4.cloned.1.call-done = f32[2,2304,256]{1,2,0:T(8,128)} async-done(((f32[2,2304,256]{1,2,0:T(8,128)}), f32[2,2304,256]{1,2,0:T(8,128)}) %all-reduce.4.cloned.1.call-update) | async-done | bytes 4718608 | tf_op jit(solution)/shard_map/psum | solution.py:22
  466.2 2.7 multiply_reduce_fusion
  468.9 1.6 fusion.8
  470.5 1.1 copy.45
  471.6 21.2 %fusion.1 = bf16[2,2304,2304]{2,1,0:T(8,128)(2,1)} fusion(bf16[2,2304,2304]{2,1,0:T(8,128)(2,1)} %param.3, pred[2]{0:T(512)(128)(4,1)S(1)} %iota_compare_fusion.3, f32[2,2304,256]{1,2,0:T(8,128)} %all-reduce.4.cloned.1.call-done, f32[2,128,2304]{2,1,0:T(8,128)} %copy-done.1, f32[2,128,2304]{2,1,0:T(8,128)S(1)} %fusion.5), kind=kOutput, calls=%fused_computation.5 | convolution fusion | flops 5494800384 | bytes 51904512 | tf_op jit(solution)/shard_map/kir,kjr->kij/dot_general | solution.py:34
  (14 shorter events, 0.2 us)
Async XLA Ops:
  7.2 57.6 %all-gather.4.cloned.1.call-start = ((), (), s32[]{:S(2)}) async-start(), calls=%async_computation | async-start | bytes 2654208 | tf_op jit(solution)/shard_map/all_gather | solution.py:59
  7.9 149.6 %all-gather.6.cloned.1.call-start = ((), (), s32[]{:S(2)}) async-start(), calls=%async_computation.2 | async-start | bytes 4718592 | tf_op jit(solution)/shard_map/all_gather | solution.py:63
  75.4 2.2 copy-start
  86.0 380.2 %all-reduce.4.cloned.1.call-start = ((), (), s32[]{:S(2)}) async-start(), calls=%async_computation.1 | async-start | bytes 9437184 | tf_op jit(solution)/shard_map/psum | solution.py:22
  283.4 1.4 copy-start.1
Sparse Core Ops, SparseCore 0:
  10.2 54.5 all-gather.3
  86.2 71.3 all-gather.5
  297.2 168.9 all-reduce.3
